TPU v7x, 32 devices: a whole 2x2x4 slice. The times are simulated.
32 devices in a mesh: rows: 8 (over y, x, core), cols: 4 (over z).
Axes of the slice: x: 2, y: 2, z: 4, core: 2. Of those that a mesh axis runs over, the one named last changes fastest.
Arguments:
- inputs: bfloat16 [2, 6144, 2048], P(None, 'rows', 'cols'), may hold values from -6 to 6
- lengths: int32 [2, 4, 3], P(None, 'cols'), may hold values from 1 to 1024, 1536 in all within a row
- gain_attn: bfloat16 [2048], P('cols'), may hold values from 0.25 to 1.75
- w_query: bfloat16 [2048, 2048], P('cols', 'rows'), may hold values from -0.125 to 0.125
- key_weight: bfloat16 [2048, 256], P('cols'), may hold values from -0.125 to 0.125
- value_weight: bfloat16 [2048, 256], P('cols'), may hold values from -0.125 to 0.125
- w_out: bfloat16 [2048, 2048], P('rows', 'cols'), may hold values from -2 to 2
- gain_ffn: bfloat16 [2048], P('cols'), may hold values from 0.25 to 1.75
- w_gate: bfloat16 [2048, 5632], P('cols', 'rows'), may hold values from -0.125 to 0.125
- w_up: bfloat16 [2048, 5632], P('cols', 'rows'), may hold values from -0.125 to 0.125
- w_down: bfloat16 [5632, 2048], P('rows', 'cols'), may hold values from -0.078125 to 0.078125
- cotangent: bfloat16 [2, 6144, 2048], P(None, 'rows', 'cols'), may hold values from -6 to 6
Outputs:
- output: bfloat16 [2, 6144, 2048], P(None, 'rows', 'cols')
- input_grad: float32 [2, 6144, 2048], P(None, 'rows', 'cols')
- grad_gain_attn: float32 [2048], P('cols')
- grad_query: float32 [2048, 2048], P('cols', 'rows')
- grad_key: float32 [2048, 256], P('cols')
- grad_value: float32 [2048, 256], P('cols')
- grad_out: float32 [2048, 2048], P('rows', 'cols')
- grad_gain_ffn: float32 [2048], P('cols')
- grad_gate: float32 [2048, 5632], P('cols', 'rows')
- grad_up: float32 [2048, 5632], P('cols', 'rows')
- grad_down: float32 [5632, 2048], P('rows', 'cols')
Inputs may be any that keep to these rules, and one draw needn't show every extreme that they name: Each row of 3 lengths sums to 1536; one length of each row is exactly 1024.
All inputs are finite; a program needn't handle non-finite values.
Results may differ from a plain program's by a relative error of at most 0.023.
Values may be sent and summed in bfloat16 or wider, within the bound.
A program may use at most 192 MiB of HBM per device.

v0:
```python
import jax
import jax.numpy as jnp
from jax import lax
from jax.sharding import PartitionSpec as P

MODEL_WIDTH = 2048
QUERY_HEADS = 32
KEY_VALUE_HEADS = 4
HEAD_SIZE = 64


eps_norm = 1e-05
rope_base = 10000.0


def slab_layout(counts, extent):
    bounds = jnp.cumsum(counts)
    places = jnp.arange(extent, dtype=jnp.int32)
    passed = (places[:, None] >= bounds[None, :]).astype(jnp.int32)
    segment = jnp.sum(passed, axis=1)
    offsets = jnp.sum(passed * counts[None, :], axis=1)
    return (segment, places - offsets)


def rope_tables(positions, head_dim):
    half_dim = head_dim // 2
    frequency = jnp.exp(
        -jnp.log(rope_base) * (2.0 * jnp.arange(half_dim, dtype=jnp.float32) / head_dim)
    )
    angles = positions.astype(jnp.float32)[:, None] * frequency[None, :]
    return (jnp.cos(angles)[:, None, :], jnp.sin(angles)[:, None, :])


def rotate(tensor, cosine_table, sine_table):
    half_dim = tensor.shape[-1] // 2
    first_half = tensor[..., :half_dim]
    second_half = tensor[..., half_dim:]
    return jnp.concatenate(
        [
            first_half * cosine_table - second_half * sine_table,
            second_half * cosine_table + first_half * sine_table,
        ],
        axis=-1,
    )


def product(left_side, right_side, transpose_right):
    if transpose_right:
        return lax.dot_general(
            left_side, right_side, (((1,), (1,)), ((), ())), preferred_element_type=jnp.float32
        )
    return jnp.dot(left_side, right_side, preferred_element_type=jnp.float32)


def outer_sum(left_side, right_side):
    return lax.dot_general(
        left_side, right_side, (((0,), (0,)), ((), ())), preferred_element_type=jnp.float32
    )


def spread_cols(gathered, weight, own_rows):

    def partial_term(first_row, row_count):
        return product(gathered, weight, False)

    return lax.psum_scatter(
        partial_term(jnp.int32(0), lax.axis_size("cols") * own_rows),
        "cols",
        scatter_dimension=0,
        tiled=True,
    )


def branch_project(gathered, local_weight, own_rows):
    return spread_cols(gathered, local_weight, own_rows)


def spread_rows(gathered, weight, own_rows):

    def partial_term(first_row, row_count):
        return product(gathered, weight, False)

    return lax.psum_scatter(
        partial_term(jnp.int32(0), lax.axis_size("rows") * own_rows),
        "rows",
        scatter_dimension=0,
        tiled=True,
    )


def grad_cols(gathered, weight, own_rows):

    def partial_term(first_row, row_count):
        return product(gathered, weight, True)

    return lax.psum_scatter(
        partial_term(jnp.int32(0), lax.axis_size("cols") * own_rows),
        "cols",
        scatter_dimension=0,
        tiled=True,
    )


def grad_rows(gathered, weight, own_rows):

    def partial_term(first_row, row_count):
        return product(gathered, weight, True)

    return lax.psum_scatter(
        partial_term(jnp.int32(0), own_rows * lax.axis_size("rows")).astype(jnp.bfloat16),
        "rows",
        scatter_dimension=0,
        tiled=True,
    ).astype(jnp.float32)


def heads_forward(block_out):
    return lax.all_gather(block_out, "cols", axis=0, tiled=True)


def heads_backward(block_grad):
    return lax.all_gather(block_grad, "cols", axis=0, tiled=True)


def grads_rows(token_grad):
    return lax.all_gather(token_grad, "rows", axis=0, tiled=True)


def normalize(residual, gain_part):
    row_totals = lax.psum(jnp.sum(residual * residual, axis=1), "cols")
    inverse_rms = lax.rsqrt(row_totals / MODEL_WIDTH + eps_norm)
    normed_input = residual * inverse_rms[:, None]
    sent_rows = (normed_input * gain_part[None, :]).astype(jnp.bfloat16)
    return (normed_input, inverse_rms, lax.all_gather(sent_rows, "rows", axis=0, tiled=True))


def norm_backward(grad_in, normed_input, inverse_rms, gain_part):
    scaled = grad_in * gain_part[None, :]
    row_dots = lax.psum(jnp.sum(scaled * normed_input, axis=1), "cols")
    grad_rows_out = inverse_rms[:, None] * (
        scaled - normed_input * (row_dots / MODEL_WIDTH)[:, None]
    )
    return (grad_rows_out, jnp.sum(grad_in * normed_input, axis=0))


def block_mask(segment, block_index, block_rows):
    places = jnp.arange(segment.shape[0], dtype=jnp.int32)
    query_places = block_index * block_rows + jnp.arange(block_rows, dtype=jnp.int32)
    query_segment = lax.dynamic_slice_in_dim(segment, block_index * block_rows, block_rows, 0)
    return (query_segment[:, None] == segment[None, :]) & (places[None, :] <= query_places[:, None])


def attention_forward(queries, key_rot, value_rows, segment):
    extent = queries.shape[0]
    block_rows = min(512, extent)
    scaling = queries.shape[-1] ** (-0.5)

    def one_block(block_index):
        query_block = lax.dynamic_slice_in_dim(queries, block_index * block_rows, block_rows, 0)
        scores = (
            jnp.einsum("qhd,kd->hqk", query_block, key_rot, preferred_element_type=jnp.float32)
            * scaling
        )
        scores = jnp.where(block_mask(segment, block_index, block_rows)[None], scores, -1e30)
        row_peak = jnp.max(scores, axis=2, keepdims=True)
        shifted = jnp.exp(scores - row_peak)
        row_total = jnp.sum(shifted, axis=2, keepdims=True)
        probs_block = (shifted / row_total).astype(jnp.bfloat16)
        mixed_out = jnp.einsum(
            "hqk,kd->qhd", probs_block, value_rows, preferred_element_type=jnp.float32
        )
        return (mixed_out.reshape(block_rows, -1), (row_peak + jnp.log(row_total))[:, :, 0])

    mixed_out, log_total = lax.map(one_block, jnp.arange(extent // block_rows, dtype=jnp.int32))
    return (mixed_out.reshape(extent, -1), log_total)


def attention_backward(queries, key_rot, value_rows, segment, log_total, grad_mixed):
    extent, heads_per_replica, head_dim = queries.shape
    block_rows = min(512, extent)
    block_count = extent // block_rows
    scaling = head_dim ** (-0.5)
    grad_blocks = grad_mixed.reshape(block_count, block_rows, heads_per_replica, head_dim)

    def one_block(totals, pieces):
        grad_keys, grad_values = totals
        block_index, grad_block, total_block = pieces
        query_block = lax.dynamic_slice_in_dim(queries, block_index * block_rows, block_rows, 0)
        scores = (
            jnp.einsum("qhd,kd->hqk", query_block, key_rot, preferred_element_type=jnp.float32)
            * scaling
        )
        scores = jnp.where(block_mask(segment, block_index, block_rows)[None], scores, -1e30)
        probs_block = jnp.exp(scores - total_block[:, :, None])
        grad_probs = jnp.einsum(
            "qhd,kd->hqk", grad_block, value_rows, preferred_element_type=jnp.float32
        )
        inner_sum = jnp.sum(grad_probs * probs_block, axis=2, keepdims=True)
        grad_scores = (probs_block * (grad_probs - inner_sum)).astype(jnp.bfloat16)
        grad_query = (
            jnp.einsum("hqk,kd->qhd", grad_scores, key_rot, preferred_element_type=jnp.float32)
            * scaling
        )
        grad_keys = (
            grad_keys
            + jnp.einsum(
                "hqk,qhd->kd", grad_scores, query_block, preferred_element_type=jnp.float32
            )
            * scaling
        )
        grad_values = grad_values + jnp.einsum(
            "hqk,qhd->kd",
            probs_block.astype(jnp.bfloat16),
            grad_block,
            preferred_element_type=jnp.float32,
        )
        return ((grad_keys, grad_values), grad_query)

    zeros_kv = jnp.zeros((extent, head_dim), jnp.float32)
    (grad_keys, grad_values), grad_query = lax.scan(
        one_block,
        (zeros_kv, zeros_kv),
        (jnp.arange(block_count, dtype=jnp.int32), grad_blocks, log_total),
    )
    return (grad_query.reshape(extent, heads_per_replica, head_dim), grad_keys, grad_values)


def local(
    inputs,
    lengths,
    gain_attn,
    w_query,
    key_weight,
    value_weight,
    w_out,
    gain_ffn,
    w_gate,
    w_up,
    w_down,
    cotangent,
):
    head_dim = HEAD_SIZE
    query_width = w_query.shape[1]
    heads_per_replica = query_width // head_dim
    local_head = lax.axis_index("rows") * heads_per_replica // (QUERY_HEADS // KEY_VALUE_HEADS)
    key_own = lax.dynamic_slice_in_dim(key_weight, local_head * head_dim, head_dim, 1)
    value_own = lax.dynamic_slice_in_dim(value_weight, local_head * head_dim, head_dim, 1)
    proj_back = jnp.concatenate([w_query, key_own, value_own], axis=1)
    proj_in = jnp.concatenate([w_query, key_weight, value_weight], axis=1)
    key_start = query_width + local_head * head_dim
    value_start = query_width + key_weight.shape[1] + local_head * head_dim
    gate_up = jnp.concatenate([w_gate, w_up], axis=1)
    ffn_width = w_gate.shape[1]
    gain_one = gain_attn.astype(jnp.float32)
    gain_two = gain_ffn.astype(jnp.float32)
    token_rows = inputs.shape[1]
    slab_rows = token_rows * lax.axis_size("rows") // lax.axis_size("cols")

    def micro_batch(totals, pieces):
        query_acc, kv_acc, out_acc, gu_acc, down_acc, gain_one_acc, gain_two_acc = totals
        block_in, counts, grad_result = pieces
        residual_in = block_in.astype(jnp.float32)
        normed_one, inverse_one, gathered_one = normalize(residual_in, gain_one)
        segment, positions = slab_layout(counts, slab_rows)
        cosine_table, sine_table = rope_tables(positions, head_dim)
        projected = branch_project(gathered_one, proj_in, slab_rows)
        queries = rotate(
            projected[:, :query_width].reshape(slab_rows, heads_per_replica, head_dim),
            cosine_table,
            sine_table,
        ).astype(jnp.bfloat16)
        key_pre = lax.dynamic_slice_in_dim(projected, key_start, head_dim, 1)
        key_rot = rotate(key_pre[:, None, :], cosine_table, sine_table)[:, 0, :].astype(
            jnp.bfloat16
        )
        value_rows = lax.dynamic_slice_in_dim(projected, value_start, head_dim, 1).astype(
            jnp.bfloat16
        )
        mixed_out, log_total = attention_forward(queries, key_rot, value_rows, segment)
        gathered_mixed = heads_forward(mixed_out.astype(jnp.bfloat16))
        hidden_state = residual_in + spread_rows(gathered_mixed, w_out, token_rows)
        normed_two, inverse_two, gathered_two = normalize(hidden_state, gain_two)
        gate_both = branch_project(gathered_two, gate_up, slab_rows)
        gate_pre = gate_both[:, :ffn_width]
        upward = gate_both[:, ffn_width:]
        gate_sigma = jax.nn.sigmoid(gate_pre)
        gathered_hidden = heads_forward((gate_pre * gate_sigma * upward).astype(jnp.bfloat16))
        result = (hidden_state + spread_rows(gathered_hidden, w_down, token_rows)).astype(
            jnp.bfloat16
        )
        gathered_grad = grads_rows(grad_result)
        down_acc = down_acc + outer_sum(gathered_hidden, gathered_grad)
        grad_hidden = grad_cols(gathered_grad, w_down, slab_rows)
        grad_gate = grad_hidden * upward * gate_sigma * (1.0 + gate_pre * (1.0 - gate_sigma))
        grad_upward = grad_hidden * gate_pre * gate_sigma
        gathered_gu = heads_backward(
            jnp.concatenate([grad_gate, grad_upward], axis=1).astype(jnp.bfloat16)
        )
        gu_acc = gu_acc + outer_sum(gathered_two, gathered_gu)
        grad_two, gain_two_part = norm_backward(
            grad_rows(gathered_gu, gate_up, token_rows), normed_two, inverse_two, gain_two
        )
        grad_state = grad_two + grad_result.astype(jnp.float32)
        gathered_state = grads_rows(grad_state.astype(jnp.bfloat16))
        out_acc = out_acc + outer_sum(gathered_mixed, gathered_state)
        grad_mixed = grad_cols(gathered_state, w_out, slab_rows).astype(jnp.bfloat16)
        grad_queries, grad_keys, grad_values = attention_backward(
            queries,
            key_rot,
            value_rows,
            segment,
            log_total,
            grad_mixed.reshape(slab_rows, heads_per_replica, head_dim),
        )
        back_queries = rotate(grad_queries, cosine_table, -sine_table).reshape(
            slab_rows, query_width
        )
        back_keys = rotate(grad_keys[:, None, :], cosine_table, -sine_table)[:, 0, :]
        gathered_proj = heads_backward(
            jnp.concatenate([back_queries, back_keys, grad_values], axis=1).astype(jnp.bfloat16)
        )
        grad_proj = outer_sum(gathered_one, gathered_proj)
        query_acc = query_acc + grad_proj[:, :query_width]
        kv_acc = kv_acc + grad_proj[:, query_width:]
        grad_one, gain_one_part = norm_backward(
            grad_rows(gathered_proj, proj_back, token_rows), normed_one, inverse_one, gain_one
        )
        grad_input = grad_one + grad_state
        new_totals = (
            query_acc,
            kv_acc,
            out_acc,
            gu_acc,
            down_acc,
            gain_one_acc + gain_one_part,
            gain_two_acc + gain_two_part,
        )
        return (new_totals, (result, grad_input))

    start_totals = (
        jnp.zeros(w_query.shape, jnp.float32),
        jnp.zeros((w_query.shape[0], 2 * head_dim), jnp.float32),
        jnp.zeros(w_out.shape, jnp.float32),
        jnp.zeros(gate_up.shape, jnp.float32),
        jnp.zeros(w_down.shape, jnp.float32),
        jnp.zeros(gain_attn.shape, jnp.float32),
        jnp.zeros(gain_ffn.shape, jnp.float32),
    )
    final_totals, stacked = lax.scan(
        micro_batch, start_totals, (inputs, lengths[:, 0, :], cotangent)
    )
    query_acc, kv_acc, out_acc, gu_acc, down_acc, gain_one_acc, gain_two_acc = final_totals
    results, grad_inputs = stacked
    key_full = lax.dynamic_update_slice_in_dim(
        jnp.zeros(key_weight.shape, jnp.float32), kv_acc[:, :head_dim], local_head * head_dim, 1
    )
    value_full = lax.dynamic_update_slice_in_dim(
        jnp.zeros(value_weight.shape, jnp.float32), kv_acc[:, head_dim:], local_head * head_dim, 1
    )
    gain_one_sum, gain_two_sum, key_sum, value_sum = (
        lax.psum(gain_one_acc.astype(jnp.bfloat16), "rows").astype(jnp.float32),
        lax.psum(gain_two_acc.astype(jnp.bfloat16), "rows").astype(jnp.float32),
        lax.psum(key_full.astype(jnp.bfloat16), "rows").astype(jnp.float32),
        lax.psum(value_full.astype(jnp.bfloat16), "rows").astype(jnp.float32),
    )
    return (
        results,
        grad_inputs,
        gain_one_sum,
        query_acc,
        key_sum,
        value_sum,
        out_acc,
        gain_two_sum,
        gu_acc[:, :ffn_width],
        gu_acc[:, ffn_width:],
        down_acc,
    )


def solution(mesh):
    in_specs = (
        P(None, "rows", "cols"),
        P(None, "cols", None),
        P("cols"),
        P("cols", "rows"),
        P("cols", None),
        P("cols", None),
        P("rows", "cols"),
        P("cols"),
        P("cols", "rows"),
        P("cols", "rows"),
        P("rows", "cols"),
        P(None, "rows", "cols"),
    )
    out_specs = (
        P(None, "rows", "cols"),
        P(None, "rows", "cols"),
        P("cols"),
        P("cols", "rows"),
        P("cols", None),
        P("cols", None),
        P("rows", "cols"),
        P("cols"),
        P("cols", "rows"),
        P("cols", "rows"),
        P("rows", "cols"),
    )
    return jax.shard_map(local, mesh=mesh, in_specs=in_specs, out_specs=out_specs, check_vma=False)
```

profile of v0, /device:TPU:0, one launch (start us, length us, event | category | flops | bytes accessed | tf_op | source)
XLA Modules:
  0.0 5168.4 jit_solution(4458208719729433427)
XLA Ops:
  17.1 5084.7 %while.87 = (s32[]{:T(128)}, f32[512,256]{1,0:T(8,128)}, f32[512,128]{1,0:T(8,128)}, f32[256,512]{1,0:T(8,128)}, f32[512,1408]{1,0:T(8,128)}, /*index=5*/f32[704...) while((s32[]{:T(128)}, f32[512,256]{1,0:T(8,128)}, ...), condition=%wide.region_29.30_spmd.clone, body=%wide.region_0.29_spmd.clone.sunk | while | flops 57317396480 | bytes 1248883840 | solution.py:349
  34.8 43.7 all-gather.13.cloned.1.call-done
  92.7 311.1 %reduce-scatter.9.cloned.1.call-done = f32[1536,768]{1,0:T(8,128)} async-done(((f32[6144,768]{1,0:T(8,128)}), f32[1536,768]{1,0:T(8,128)}) %reduce-scatter.9.cloned.1.call-update) | async-done | bytes 4718608 | tf_op jit(solution)/shard_map/while/body/eval_jaxpr/reduce_scatter | solution.py:66
  454.2 64.5 %all-gather.17.cloned.1.call-done = bf16[6144,256]{1,0:T(8,128)(2,1)} async-done(((bf16[1536,256]{1,0:T(8,128)(2,1)}), bf16[6144,256]{1,0:T(8,128)(2,1)}) %all-gather.17.cloned.1.call-update) | async-done | bytes 3145744 | tf_op jit(solution)/shard_map/while/body/eval_jaxpr/all_gather | solution.py:118
  529.4 88.7 %reduce-scatter.13.cloned.1.call-done = f32[768,512]{1,0:T(8,128)} async-done(((f32[6144,512]{1,0:T(8,128)}), f32[768,512]{1,0:T(8,128)}) %reduce-scatter.13.cloned.1.call-update) | async-done | bytes 1572880 | tf_op jit(solution)/shard_map/while/body/eval_jaxpr/reduce_scatter | solution.py:83
  731.9 272.3 %reduce-scatter.11.cloned.1.call-done = f32[1536,704]{0,1:T(8,128)} async-done(((f32[6144,704]{0,1:T(8,128)}), f32[1536,704]{0,1:T(8,128)}) %reduce-scatter.11.cloned.1.call-update) | async-done | bytes 4325392 | tf_op jit(solution)/shard_map/while/body/eval_jaxpr/reduce_scatter | solution.py:96
  1004.2 572.1 %reduce-scatter.15.cloned.1.call-done = f32[1536,1408]{0,1:T(8,128)} async-done(((f32[6144,1408]{0,1:T(8,128)}), f32[1536,1408]{0,1:T(8,128)}) %reduce-scatter.15.cloned.1.call-update) | async-done | bytes 8650768 | tf_op jit(solution)/shard_map/while/body/eval_jaxpr/reduce_scatter | solution.py:66
  1586.1 297.5 %all-gather.21.cloned.1.call-done = bf16[6144,1408]{0,1:T(8,128)(2,1)} async-done(((bf16[1536,1408]{0,1:T(8,128)(2,1)}), bf16[6144,1408]{0,1:T(8,128)(2,1)}) %all-gather.21.cloned.1.call-update) | async-done | bytes 17301520 | tf_op jit(solution)/shard_map/while/body/eval_jaxpr/all_gather | solution.py:122
  1899.5 60.9 %reduce-scatter.17.cloned.1.call-done = bf16[768,512]{1,0:T(8,128)(2,1)} async-done(((bf16[6144,512]{1,0:T(8,128)(2,1)}), bf16[768,512]{1,0:T(8,128)(2,1)}) %reduce-scatter.17.cloned.1.call-update) | async-done | bytes 786448 | tf_op jit(solution)/shard_map/while/body/eval_jaxpr/reduce_scatter | solution.py:109
  1977.3 42.7 all-gather.23.cloned.1.call-done
  2028.3 109.9 %reduce-scatter.19.cloned.1.call-done = f32[1536,256]{1,0:T(8,128)} async-done(((f32[6144,256]{1,0:T(8,128)}), f32[1536,256]{1,0:T(8,128)}) %reduce-scatter.19.cloned.1.call-update) | async-done | bytes 1572880 | tf_op jit(solution)/shard_map/while/body/eval_jaxpr/reduce_scatter | solution.py:96
  2145.4 94.6 %while.89 = (s32[]{:T(128)}, f32[1536,64]{0,1:T(8,128)}, f32[1536,64]{0,1:T(8,128)S(1)}, f32[3,512,4,64]{1,0,3,2:T(4,128)}, s32[3]{0:T(128)S(1)}, /*index=5*/s32...) while((s32[]{:T(128)}, f32[1536,64]{0,1:T(8,128)}, ...), condition=%wide.region_22.22_spmd.clone, body=%wide.region_20.21_spmd.clone.sunk | while | flops 2044557824 | bytes 130146640 | solution.py:220
  2245.8 48.4 all-gather.27.cloned.1.call-done
  2305.9 77.9 %all-gather.25.cloned.1.call-done = bf16[6144,384]{0,1:T(8,128)(2,1)} async-done(((bf16[1536,384]{0,1:T(8,128)(2,1)}), bf16[6144,384]{0,1:T(8,128)(2,1)}) %all-gather.25.cloned.1.call-update) | async-done | bytes 4718608 | tf_op jit(solution)/shard_map/while/body/eval_jaxpr/all_gather | solution.py:122
  2423.3 54.6 %reduce-scatter.23.cloned.1.call-done = f32[768,512]{1,0:T(8,128)} async-done(((f32[6144,512]{1,0:T(8,128)}), f32[768,512]{1,0:T(8,128)}) %reduce-scatter.23.cloned.1.call-update) | async-done | bytes 1572880 | tf_op jit(solution)/shard_map/while/body/eval_jaxpr/reduce_scatter | solution.py:83
  2491.5 51.5 reduce-scatter.21.cloned.1.call-done
  2573.0 44.2 all-gather.13.cloned.1.call-done
  2631.2 311.2 %reduce-scatter.9.cloned.1.call-done = f32[1536,768]{1,0:T(8,128)} async-done(((f32[6144,768]{1,0:T(8,128)}), f32[1536,768]{1,0:T(8,128)}) %reduce-scatter.9.cloned.1.call-update) | async-done | bytes 4718608 | tf_op jit(solution)/shard_map/while/body/eval_jaxpr/reduce_scatter | solution.py:66
  2950.6 41.3 while.88
  2992.8 64.5 %all-gather.17.cloned.1.call-done = bf16[6144,256]{1,0:T(8,128)(2,1)} async-done(((bf16[1536,256]{1,0:T(8,128)(2,1)}), bf16[6144,256]{1,0:T(8,128)(2,1)}) %all-gather.17.cloned.1.call-update) | async-done | bytes 3145744 | tf_op jit(solution)/shard_map/while/body/eval_jaxpr/all_gather | solution.py:118
  3068.0 88.7 %reduce-scatter.13.cloned.1.call-done = f32[768,512]{1,0:T(8,128)} async-done(((f32[6144,512]{1,0:T(8,128)}), f32[768,512]{1,0:T(8,128)}) %reduce-scatter.13.cloned.1.call-update) | async-done | bytes 1572880 | tf_op jit(solution)/shard_map/while/body/eval_jaxpr/reduce_scatter | solution.py:83
  3270.8 272.3 %reduce-scatter.11.cloned.1.call-done = f32[1536,704]{0,1:T(8,128)} async-done(((f32[6144,704]{0,1:T(8,128)}), f32[1536,704]{0,1:T(8,128)}) %reduce-scatter.11.cloned.1.call-update) | async-done | bytes 4325392 | tf_op jit(solution)/shard_map/while/body/eval_jaxpr/reduce_scatter | solution.py:96
  3543.1 571.9 %reduce-scatter.15.cloned.1.call-done = f32[1536,1408]{0,1:T(8,128)} async-done(((f32[6144,1408]{0,1:T(8,128)}), f32[1536,1408]{0,1:T(8,128)}) %reduce-scatter.15.cloned.1.call-update) | async-done | bytes 8650768 | tf_op jit(solution)/shard_map/while/body/eval_jaxpr/reduce_scatter | solution.py:66
  4124.8 297.5 %all-gather.21.cloned.1.call-done = bf16[6144,1408]{0,1:T(8,128)(2,1)} async-done(((bf16[1536,1408]{0,1:T(8,128)(2,1)}), bf16[6144,1408]{0,1:T(8,128)(2,1)}) %all-gather.21.cloned.1.call-update) | async-done | bytes 17301520 | tf_op jit(solution)/shard_map/while/body/eval_jaxpr/all_gather | solution.py:122
  4438.2 60.9 %reduce-scatter.17.cloned.1.call-done = bf16[768,512]{1,0:T(8,128)(2,1)} async-done(((bf16[6144,512]{1,0:T(8,128)(2,1)}), bf16[768,512]{1,0:T(8,128)(2,1)}) %reduce-scatter.17.cloned.1.call-update) | async-done | bytes 786448 | tf_op jit(solution)/shard_map/while/body/eval_jaxpr/reduce_scatter | solution.py:109
  4516.0 42.7 all-gather.23.cloned.1.call-done
  4567.0 109.9 %reduce-scatter.19.cloned.1.call-done = f32[1536,256]{1,0:T(8,128)} async-done(((f32[6144,256]{1,0:T(8,128)}), f32[1536,256]{1,0:T(8,128)}) %reduce-scatter.19.cloned.1.call-update) | async-done | bytes 1572880 | tf_op jit(solution)/shard_map/while/body/eval_jaxpr/reduce_scatter | solution.py:96
  4684.1 94.7 %while.89 = (s32[]{:T(128)}, f32[1536,64]{0,1:T(8,128)}, f32[1536,64]{0,1:T(8,128)S(1)}, f32[3,512,4,64]{1,0,3,2:T(4,128)}, s32[3]{0:T(128)S(1)}, /*index=5*/s32...) while((s32[]{:T(128)}, f32[1536,64]{0,1:T(8,128)}, ...), condition=%wide.region_22.22_spmd.clone, body=%wide.region_20.21_spmd.clone.sunk | while | flops 2044557824 | bytes 130146640 | solution.py:220
  4784.6 48.4 all-gather.27.cloned.1.call-done
  4844.7 77.9 %all-gather.25.cloned.1.call-done = bf16[6144,384]{0,1:T(8,128)(2,1)} async-done(((bf16[1536,384]{0,1:T(8,128)(2,1)}), bf16[6144,384]{0,1:T(8,128)(2,1)}) %all-gather.25.cloned.1.call-update) | async-done | bytes 4718608 | tf_op jit(solution)/shard_map/while/body/eval_jaxpr/all_gather | solution.py:122
  4962.4 54.4 %reduce-scatter.23.cloned.1.call-done = f32[768,512]{1,0:T(8,128)} async-done(((f32[6144,512]{1,0:T(8,128)}), f32[768,512]{1,0:T(8,128)}) %reduce-scatter.23.cloned.1.call-update) | async-done | bytes 1572880 | tf_op jit(solution)/shard_map/while/body/eval_jaxpr/reduce_scatter | solution.py:83
  5030.3 51.7 reduce-scatter.21.cloned.1.call-done
  (609 shorter events, 988.3 us)
Async XLA Ops:
  17.1 61.5 %all-gather.13.cloned.1.call-start = ((), (), s32[]{:S(2)}) async-start(), calls=%async_computation.9 | async-start | bytes 7077888 | tf_op jit(solution)/shard_map/while/body/eval_jaxpr/all_gather | solution.py:134
  34.8 369.0 %reduce-scatter.9.cloned.1.call-start = ((), (), s32[]{:S(2)}) async-start(), calls=%async_computation.10 | async-start | bytes 23592960 | tf_op jit(solution)/shard_map/while/body/eval_jaxpr/reduce_scatter | solution.py:66
  89.8 429.0 %all-gather.17.cloned.1.call-start = ((), (), s32[]{:S(2)}) async-start(), calls=%async_computation.13 | async-start | bytes 3932160 | tf_op jit(solution)/shard_map/while/body/eval_jaxpr/all_gather | solution.py:118
  454.2 163.9 %reduce-scatter.13.cloned.1.call-start = ((), (), s32[]{:S(2)}) async-start(), calls=%async_computation.14 | async-start | bytes 14155776 | tf_op jit(solution)/shard_map/while/body/eval_jaxpr/reduce_scatter | solution.py:83
  527.0 138.8 %all-gather.15.cloned.1.call-start = ((), (), s32[]{:S(2)}) async-start(), calls=%async_computation.11 | async-start | bytes 7077888 | tf_op jit(solution)/shard_map/while/body/eval_jaxpr/all_gather | solution.py:126
  529.4 183.6 %all-gather.19.cloned.1.call-start = ((), (), s32[]{:S(2)}) async-start(), calls=%async_computation.15 | async-start | bytes 7077888 | tf_op jit(solution)/shard_map/while/body/eval_jaxpr/all_gather | solution.py:134
  632.8 371.4 %reduce-scatter.11.cloned.1.call-start = ((), (), s32[]{:S(2)}) async-start(), calls=%async_computation.12 | async-start | bytes 21626880 | tf_op jit(solution)/shard_map/while/body/eval_jaxpr/reduce_scatter | solution.py:96
  679.9 896.4 %reduce-scatter.15.cloned.1.call-start = ((), (), s32[]{:S(2)}) async-start(), calls=%async_computation.16 | async-start | bytes 43253760 | tf_op jit(solution)/shard_map/while/body/eval_jaxpr/reduce_scatter | solution.py:66
  731.8 1151.8 %all-gather.21.cloned.1.call-start = ((), (), s32[]{:S(2)}) async-start(), calls=%async_computation.17 | async-start | bytes 21626880 | tf_op jit(solution)/shard_map/while/body/eval_jaxpr/all_gather | solution.py:122
  1585.9 374.5 %reduce-scatter.17.cloned.1.call-start = ((), (), s32[]{:S(2)}) async-start(), calls=%async_computation.18 | async-start | bytes 7077888 | tf_op jit(solution)/shard_map/while/body/eval_jaxpr/reduce_scatter | solution.py:109
  1899.5 120.5 %all-gather.23.cloned.1.call-start = ((), (), s32[]{:S(2)}) async-start(), calls=%async_computation.19 | async-start | bytes 7077888 | tf_op jit(solution)/shard_map/while/body/eval_jaxpr/all_gather | solution.py:126
  1977.2 161.0 %reduce-scatter.19.cloned.1.call-start = ((), (), s32[]{:S(2)}) async-start(), calls=%async_computation.20 | async-start | bytes 7864320 | tf_op jit(solution)/shard_map/while/body/eval_jaxpr/reduce_scatter | solution.py:96
  2027.3 267.0 %all-gather.27.cloned.1.call-start = ((), (), s32[]{:S(2)}) async-start(), calls=%async_computation.22 | async-start | bytes 10813440 | tf_op jit(solution)/shard_map/while/body/eval_jaxpr/all_gather | solution.py:118
  2028.0 355.8 %all-gather.25.cloned.1.call-start = ((), (), s32[]{:S(2)}) async-start(), calls=%async_computation.21 | async-start | bytes 5898240 | tf_op jit(solution)/shard_map/while/body/eval_jaxpr/all_gather | solution.py:122
  2245.7 232.2 %reduce-scatter.23.cloned.1.call-start = ((), (), s32[]{:S(2)}) async-start(), calls=%async_computation.24 | async-start | bytes 14155776 | tf_op jit(solution)/shard_map/while/body/eval_jaxpr/reduce_scatter | solution.py:83
  2305.9 237.1 %reduce-scatter.21.cloned.1.call-start = ((), (), s32[]{:S(2)}) async-start(), calls=%async_computation.23 | async-start | bytes 7077888 | tf_op jit(solution)/shard_map/while/body/eval_jaxpr/reduce_scatter | solution.py:109
  2560.2 56.9 %all-gather.13.cloned.1.call-start = ((), (), s32[]{:S(2)}) async-start(), calls=%async_computation.9 | async-start | bytes 7077888 | tf_op jit(solution)/shard_map/while/body/eval_jaxpr/all_gather | solution.py:134
  2572.9 369.5 %reduce-scatter.9.cloned.1.call-start = ((), (), s32[]{:S(2)}) async-start(), calls=%async_computation.10 | async-start | bytes 23592960 | tf_op jit(solution)/shard_map/while/body/eval_jaxpr/reduce_scatter | solution.py:66
  2628.3 429.0 %all-gather.17.cloned.1.call-start = ((), (), s32[]{:S(2)}) async-start(), calls=%async_computation.13 | async-start | bytes 3932160 | tf_op jit(solution)/shard_map/while/body/eval_jaxpr/all_gather | solution.py:118
  2992.8 163.9 %reduce-scatter.13.cloned.1.call-start = ((), (), s32[]{:S(2)}) async-start(), calls=%async_computation.14 | async-start | bytes 14155776 | tf_op jit(solution)/shard_map/while/body/eval_jaxpr/reduce_scatter | solution.py:83
  3065.6 139.0 %all-gather.15.cloned.1.call-start = ((), (), s32[]{:S(2)}) async-start(), calls=%async_computation.11 | async-start | bytes 7077888 | tf_op jit(solution)/shard_map/while/body/eval_jaxpr/all_gather | solution.py:126
  3067.9 183.9 %all-gather.19.cloned.1.call-start = ((), (), s32[]{:S(2)}) async-start(), calls=%async_computation.15 | async-start | bytes 7077888 | tf_op jit(solution)/shard_map/while/body/eval_jaxpr/all_gather | solution.py:134
  3171.4 371.7 %reduce-scatter.11.cloned.1.call-start = ((), (), s32[]{:S(2)}) async-start(), calls=%async_computation.12 | async-start | bytes 21626880 | tf_op jit(solution)/shard_map/while/body/eval_jaxpr/reduce_scatter | solution.py:96
  3218.7 896.4 %reduce-scatter.15.cloned.1.call-start = ((), (), s32[]{:S(2)}) async-start(), calls=%async_computation.16 | async-start | bytes 43253760 | tf_op jit(solution)/shard_map/while/body/eval_jaxpr/reduce_scatter | solution.py:66
  3270.7 1151.6 %all-gather.21.cloned.1.call-start = ((), (), s32[]{:S(2)}) async-start(), calls=%async_computation.17 | async-start | bytes 21626880 | tf_op jit(solution)/shard_map/while/body/eval_jaxpr/all_gather | solution.py:122
  4124.6 374.5 %reduce-scatter.17.cloned.1.call-start = ((), (), s32[]{:S(2)}) async-start(), calls=%async_computation.18 | async-start | bytes 7077888 | tf_op jit(solution)/shard_map/while/body/eval_jaxpr/reduce_scatter | solution.py:109
  4438.2 120.5 %all-gather.23.cloned.1.call-start = ((), (), s32[]{:S(2)}) async-start(), calls=%async_computation.19 | async-start | bytes 7077888 | tf_op jit(solution)/shard_map/while/body/eval_jaxpr/all_gather | solution.py:126
  4515.9 161.0 %reduce-scatter.19.cloned.1.call-start = ((), (), s32[]{:S(2)}) async-start(), calls=%async_computation.20 | async-start | bytes 7864320 | tf_op jit(solution)/shard_map/while/body/eval_jaxpr/reduce_scatter | solution.py:96
  4566.0 267.0 %all-gather.27.cloned.1.call-start = ((), (), s32[]{:S(2)}) async-start(), calls=%async_computation.22 | async-start | bytes 10813440 | tf_op jit(solution)/shard_map/while/body/eval_jaxpr/all_gather | solution.py:118
  4566.7 355.8 %all-gather.25.cloned.1.call-start = ((), (), s32[]{:S(2)}) async-start(), calls=%async_computation.21 | async-start | bytes 5898240 | tf_op jit(solution)/shard_map/while/body/eval_jaxpr/all_gather | solution.py:122
  4784.5 232.3 %reduce-scatter.23.cloned.1.call-start = ((), (), s32[]{:S(2)}) async-start(), calls=%async_computation.24 | async-start | bytes 14155776 | tf_op jit(solution)/shard_map/while/body/eval_jaxpr/reduce_scatter | solution.py:83
  4844.6 237.4 %reduce-scatter.21.cloned.1.call-start = ((), (), s32[]{:S(2)}) async-start(), calls=%async_computation.23 | async-start | bytes 7077888 | tf_op jit(solution)/shard_map/while/body/eval_jaxpr/reduce_scatter | solution.py:109
  (115 other events, 9632.3 us)
Sparse Core Ops, SparseCore 0:
  34.9 43.5 all-gather.12
  89.9 313.9 reduce-scatter.8
  454.3 64.3 all-gather.16
  527.1 90.9 reduce-scatter.12
  620.4 45.3 all-gather.14
  667.6 45.3 all-gather.18
  715.4 288.7 reduce-scatter.10
  1006.6 569.6 reduce-scatter.14
  1586.0 297.5 all-gather.20
  1899.6 60.7 reduce-scatter.16
  1977.3 42.6 all-gather.22
  2027.4 110.7 reduce-scatter.18
  2139.8 154.4 all-gather.26
  2296.2 87.5 all-gather.24
  2387.2 90.7 reduce-scatter.22
  2481.2 61.7 reduce-scatter.20
  2573.0 44.0 all-gather.12
  2628.5 313.9 reduce-scatter.8
  2992.9 64.3 all-gather.16
  3065.7 90.9 reduce-scatter.12
  3159.1 45.3 all-gather.14
  3206.5 45.3 all-gather.18
  3254.3 288.7 reduce-scatter.10
  3545.3 569.6 reduce-scatter.14
  4124.7 297.5 all-gather.20
  4438.3 60.7 reduce-scatter.16
  4516.1 42.6 all-gather.22
  4566.1 110.7 reduce-scatter.18
  4678.5 154.4 all-gather.26
  4834.9 87.5 all-gather.24
  4926.1 90.7 reduce-scatter.22
  5020.2 61.7 reduce-scatter.20
Sparse Core Ops, SparseCore 1:
  5105.9 51.5 all-reduce.3
where the time goes:
time: 5170 us
  waiting for transfers between devices  4360 us (84%)
  matrix products  385 us (7%)
  other arithmetic  145 us (3%)
  local copies, waits for them, and re-layouts  142 us (3%)
  blocking collectives  104 us (2%)
    reduce_scatter x4, waiting for transfers between devices, spread_cols(): lax.psum_scatter(partial_term(jnp.int32(0), lax.axis_size('cols') * own_r...  1770 us
    reduce_scatter x4, waiting for transfers between devices, grad_cols(): lax.psum_scatter(partial_term(jnp.int32(0), lax.axis_size('cols') * own_r...  765 us
    all_gather x4, waiting for transfers between devices, heads_backward(): return lax.all_gather(block_grad, 'cols', axis=0, tiled=True)  751 us
    reduce_scatter x4, waiting for transfers between devices, spread_rows(): lax.psum_scatter(partial_term(jnp.int32(0), lax.axis_size('rows') * own_r...  286 us
    all_gather x4, waiting for transfers between devices, heads_forward(): return lax.all_gather(block_out, 'cols', axis=0, tiled=True)  226 us
    reduce_scatter x4, waiting for transfers between devices, grad_rows(): lax.psum_scatter(partial_term(jnp.int32(0), own_rows * lax.axis_size('row...  225 us
    all_gather x4, waiting for transfers between devices, normalize(): lax.all_gather(sent_rows, 'rows', axis=0, tiled=True)  154 us
    all_gather x4, waiting for transfers between devices, grads_rows(): return lax.all_gather(token_grad, 'rows', axis=0, tiled=True)  150 us
  transfers between devices with their start and end apart: 33, of which 33 were waited for; matrix products, arithmetic and copies ran while one was open for 8% of the time, Pallas kernels for 0%

commit v1 on v0

v1 whole, which is shorter than its diff:
```python
import jax
import jax.numpy as jnp
from jax import lax
from jax.sharding import PartitionSpec as P

QUERY_HEADS = 32
KEY_VALUE_HEADS = 4
HEAD_SIZE = 64
QUERY_ROWS = 512

eps_norm = 1e-05
rope_base = 10000.0
F32 = jnp.float32
BF16 = jnp.bfloat16


def slab_layout(counts, extent):
    bounds = jnp.cumsum(counts)
    places = jnp.arange(extent, dtype=jnp.int32)
    passed = (places[:, None] >= bounds[None, :]).astype(jnp.int32)
    segment = jnp.sum(passed, axis=1)
    offsets = jnp.sum(passed * counts[None, :], axis=1)
    return (segment, places - offsets)


def rope_tables(positions, head_dim):
    half_dim = head_dim // 2
    frequency = jnp.exp(
        -jnp.log(rope_base) * (2.0 * jnp.arange(half_dim, dtype=F32) / head_dim)
    )
    angles = positions.astype(F32)[:, None] * frequency[None, :]
    return (jnp.cos(angles)[:, None, :], jnp.sin(angles)[:, None, :])


def rotate(tensor, cosine_table, sine_table):
    half_dim = tensor.shape[-1] // 2
    first_half = tensor[..., :half_dim]
    second_half = tensor[..., half_dim:]
    return jnp.concatenate(
        [
            first_half * cosine_table - second_half * sine_table,
            second_half * cosine_table + first_half * sine_table,
        ],
        axis=-1,
    )


def dot_nn(left_side, right_side, out=F32):
    return lax.dot_general(
        left_side, right_side, (((1,), (0,)), ((), ())), preferred_element_type=F32
    ).astype(out)


def dot_nt(left_side, right_side, out=F32):
    return lax.dot_general(
        left_side, right_side, (((1,), (1,)), ((), ())), preferred_element_type=F32
    ).astype(out)


def dot_tn(left_side, right_side):
    return lax.dot_general(
        left_side, right_side, (((0,), (0,)), ((), ())), preferred_element_type=F32
    )


def gather_rows(part):
    return lax.all_gather(part, "rows", axis=0, tiled=True)


def scatter_rows(partial_sum):
    return lax.psum_scatter(partial_sum, "rows", scatter_dimension=0, tiled=True).astype(F32)


def gather_cols(part):
    return lax.all_gather(part, "cols", axis=0, tiled=True)


def scatter_cols(partial_sum):
    return lax.psum_scatter(
        partial_sum.astype(BF16), "cols", scatter_dimension=0, tiled=True
    ).astype(F32)


def to_tokens(array, n_rows, n_cols):
    own_rows, own_features = array.shape
    lead = array.reshape(n_rows, own_rows // n_rows, own_features)
    lead = lax.all_to_all(lead, "rows", 0, 0, tiled=True)
    lead = lead.reshape(n_cols, own_rows // n_cols, own_features)
    lead = lax.all_to_all(lead, "cols", 0, 0, tiled=True)
    return jnp.transpose(lead, (1, 0, 2)).reshape(own_rows // n_cols, n_cols * own_features)


def from_tokens(array, n_rows, n_cols):
    few_rows, features = array.shape
    lead = jnp.transpose(array.reshape(few_rows, n_cols, features // n_cols), (1, 0, 2))
    lead = lax.all_to_all(lead, "cols", 0, 0, tiled=True)
    lead = lead.reshape(n_rows, few_rows * n_cols // n_rows, features // n_cols)
    lead = lax.all_to_all(lead, "rows", 0, 0, tiled=True)
    return lead.reshape(few_rows * n_cols, features // n_cols)


def key_mask(segment, first, block_rows):
    last = first + block_rows
    query_places = first + jnp.arange(block_rows, dtype=jnp.int32)
    places = jnp.arange(last, dtype=jnp.int32)
    same = segment[first:last, None] == segment[None, :last]
    return same & (places[None, :] <= query_places[:, None])


def attention_forward(queries, key_rot, value_rows, segment):
    extent = queries.shape[1]
    block_rows = min(QUERY_ROWS, extent)
    scaling = queries.shape[-1] ** (-0.5)
    outs, totals = [], []
    for first in range(0, extent, block_rows):
        last = first + block_rows
        scores = (
            jnp.einsum(
                "hqd,kd->hqk",
                queries[:, first:last],
                key_rot[:last],
                preferred_element_type=F32,
            )
            * scaling
        )
        scores = jnp.where(key_mask(segment, first, block_rows)[None], scores, -1e30)
        row_peak = jnp.max(scores, axis=2, keepdims=True)
        shifted = jnp.exp(scores - row_peak)
        row_total = jnp.sum(shifted, axis=2, keepdims=True)
        probs = (shifted / row_total).astype(BF16)
        outs.append(
            jnp.einsum("hqk,kd->qhd", probs, value_rows[:last], preferred_element_type=F32)
        )
        totals.append(row_peak + jnp.log(row_total))
    return (jnp.concatenate(outs, axis=0).astype(BF16), totals)


def attention_backward(queries, key_rot, value_rows, segment, totals, grad_mixed):
    heads, extent, head_dim = queries.shape
    block_rows = min(QUERY_ROWS, extent)
    scaling = head_dim ** (-0.5)
    grad_queries = []
    grad_keys = jnp.zeros((extent, head_dim), F32)
    grad_values = jnp.zeros((extent, head_dim), F32)
    for first, total in zip(range(0, extent, block_rows), totals):
        last = first + block_rows
        query_block = queries[:, first:last]
        grad_block = grad_mixed[:, first:last]
        keys, values = key_rot[:last], value_rows[:last]
        scores = (
            jnp.einsum("hqd,kd->hqk", query_block, keys, preferred_element_type=F32) * scaling
        )
        scores = jnp.where(key_mask(segment, first, block_rows)[None], scores, -1e30)
        probs = jnp.exp(scores - total)
        grad_probs = jnp.einsum("hqd,kd->hqk", grad_block, values, preferred_element_type=F32)
        inner_sum = jnp.sum(grad_probs * probs, axis=2, keepdims=True)
        grad_scores = (probs * (grad_probs - inner_sum)).astype(BF16)
        grad_queries.append(
            jnp.einsum("hqk,kd->qhd", grad_scores, keys, preferred_element_type=F32) * scaling
        )
        rest = ((0, extent - last), (0, 0))
        grad_keys = grad_keys + jnp.pad(
            jnp.einsum("hqk,hqd->kd", grad_scores, query_block, preferred_element_type=F32)
            * scaling,
            rest,
        )
        grad_values = grad_values + jnp.pad(
            jnp.einsum(
                "hqk,hqd->kd", probs.astype(BF16), grad_block, preferred_element_type=F32
            ),
            rest,
        )
    return (jnp.concatenate(grad_queries, axis=0), grad_keys, grad_values)


def norm_backward(grad_in, normed, inverse_rms, gain):
    scaled = grad_in * gain[None, :]
    row_mean = jnp.mean(scaled * normed, axis=1, keepdims=True)
    return (
        inverse_rms * (scaled - normed * row_mean),
        jnp.sum(grad_in * normed, axis=0),
    )


def local(
    inputs,
    lengths,
    gain_attn,
    w_query,
    key_weight,
    value_weight,
    w_out,
    gain_ffn,
    w_gate,
    w_up,
    w_down,
    cotangent,
):
    n_rows, n_cols = lax.axis_size("rows"), lax.axis_size("cols")
    batches, own_rows, _ = inputs.shape
    sub_rows = own_rows // n_rows
    per_block = n_rows // n_cols
    slab_rows = own_rows * n_rows // n_cols
    head_dim = HEAD_SIZE
    query_width = w_query.shape[1]
    ffn_width = w_gate.shape[1]
    heads = query_width // head_dim
    proj_width = query_width + 2 * head_dim
    local_head = lax.axis_index("rows") * heads // (QUERY_HEADS // KEY_VALUE_HEADS)
    key_own = lax.dynamic_slice_in_dim(key_weight, local_head * head_dim, head_dim, 1)
    value_own = lax.dynamic_slice_in_dim(value_weight, local_head * head_dim, head_dim, 1)

    def ordered(array):
        wide = array.reshape(n_rows, per_block, sub_rows, -1)
        return jnp.transpose(wide, (1, 0, 2, 3)).reshape(slab_rows, -1)

    def reordered(array):
        wide = array.reshape(per_block, n_rows, sub_rows, -1)
        return jnp.transpose(wide, (1, 0, 2, 3)).reshape(slab_rows, -1)

    def by_head(array):
        return jnp.transpose(array.reshape(slab_rows, heads, head_dim), (1, 0, 2))

    rows_in = [to_tokens(inputs[m], n_rows, n_cols) for m in range(batches)]
    packed = gather_cols(
        jnp.concatenate(
            [w_query, key_own, value_own, gain_attn[:, None], gain_ffn[:, None]], axis=1
        )
    )
    proj_w = packed[:, :proj_width]
    gain_one = packed[:, proj_width].astype(F32)
    gain_two = packed[:, proj_width + 1].astype(F32)
    out_w = gather_cols(w_out.T)
    gate_up_w = gather_cols(jnp.concatenate([w_gate, w_up], axis=1))
    down_w = gather_cols(w_down.T)
    rows_dy = [to_tokens(cotangent[m], n_rows, n_cols) for m in range(batches)]

    kept = []
    results = []
    for m in range(batches):
        row_in = rows_in[m].astype(F32)
        inverse_one = lax.rsqrt(jnp.mean(row_in * row_in, axis=1, keepdims=True) + eps_norm)
        normed_one = row_in * inverse_one
        all_one = gather_rows((normed_one * gain_one[None, :]).astype(BF16))
        segment, positions = slab_layout(lengths[m, 0], slab_rows)
        cosine_table, sine_table = rope_tables(positions, head_dim)
        projected = ordered(dot_nn(all_one, proj_w))
        queries = rotate(
            projected[:, :query_width].reshape(slab_rows, heads, head_dim),
            cosine_table,
            sine_table,
        ).astype(BF16)
        queries = jnp.transpose(queries, (1, 0, 2))
        key_rot = rotate(
            projected[:, None, query_width : query_width + head_dim], cosine_table, sine_table
        )[:, 0].astype(BF16)
        value_rows = projected[:, query_width + head_dim :].astype(BF16)
        mixed, totals = attention_forward(queries, key_rot, value_rows, segment)
        mixed = reordered(mixed.reshape(slab_rows, query_width))
        hidden_state = row_in + scatter_rows(dot_nt(mixed, out_w, BF16))
        inverse_two = lax.rsqrt(
            jnp.mean(hidden_state * hidden_state, axis=1, keepdims=True) + eps_norm
        )
        normed_two = hidden_state * inverse_two
        all_two = gather_rows((normed_two * gain_two[None, :]).astype(BF16))
        gate_both = dot_nn(all_two, gate_up_w)
        gate_pre, upward = gate_both[:, :ffn_width], gate_both[:, ffn_width:]
        gate_sigma = jax.nn.sigmoid(gate_pre)
        hidden = (gate_pre * gate_sigma * upward).astype(BF16)
        result = hidden_state + scatter_rows(dot_nt(hidden, down_w, BF16))
        results.append(from_tokens(result.astype(BF16), n_rows, n_cols))
        kept.append(
            (
                all_one, normed_one, inverse_one, segment, cosine_table, sine_table,
                queries, key_rot, value_rows, mixed, totals, normed_two, inverse_two,
                all_two, gate_both, hidden,
            )
        )

    sums = None
    grad_inputs = []
    for m in range(batches):
        (
            all_one, normed_one, inverse_one, segment, cosine_table, sine_table,
            queries, key_rot, value_rows, mixed, totals, normed_two, inverse_two,
            all_two, gate_both, hidden,
        ) = kept[m]
        all_dy = gather_rows(rows_dy[m])
        grad_down = dot_tn(all_dy, hidden)
        grad_hidden = dot_nn(all_dy, down_w)
        gate_pre, upward = gate_both[:, :ffn_width], gate_both[:, ffn_width:]
        gate_sigma = jax.nn.sigmoid(gate_pre)
        grad_gate = grad_hidden * upward * gate_sigma * (1.0 + gate_pre * (1.0 - gate_sigma))
        grad_up = grad_hidden * gate_pre * gate_sigma
        grad_both = jnp.concatenate([grad_gate.astype(BF16), grad_up.astype(BF16)], axis=1)
        grad_gu = dot_tn(all_two, grad_both)
        grad_two, gain_two_part = norm_backward(
            scatter_rows(dot_nt(grad_both, gate_up_w, BF16)), normed_two, inverse_two, gain_two
        )
        grad_state = grad_two + rows_dy[m].astype(F32)
        all_dh = gather_rows(grad_state.astype(BF16))
        grad_out = dot_tn(all_dh, mixed)
        grad_mixed = by_head(ordered(dot_nn(all_dh, out_w, BF16)))
        grad_q, grad_k, grad_v = attention_backward(
            queries, key_rot, value_rows, segment, totals, grad_mixed
        )
        back_q = rotate(grad_q, cosine_table, -sine_table).reshape(slab_rows, query_width)
        back_k = rotate(grad_k[:, None, :], cosine_table, -sine_table)[:, 0, :]
        grad_qkv = reordered(jnp.concatenate([back_q, back_k, grad_v], axis=1).astype(BF16))
        grad_proj = dot_tn(all_one, grad_qkv)
        grad_one, gain_one_part = norm_backward(
            scatter_rows(dot_nt(grad_qkv, proj_w, BF16)), normed_one, inverse_one, gain_one
        )
        grad_inputs.append(
            from_tokens((grad_one + grad_state).astype(BF16), n_rows, n_cols).astype(F32)
        )
        terms = (
            grad_down,
            grad_gu,
            grad_out,
            jnp.concatenate(
                [grad_proj, gain_one_part[:, None], gain_two_part[:, None]], axis=1
            ),
        )
        sums = terms if sums is None else tuple(a + b for a, b in zip(sums, terms))

    grad_down = scatter_cols(sums[0])
    grad_gu = scatter_cols(sums[1])
    grad_out = scatter_cols(sums[2])
    grad_proj = scatter_cols(sums[3])
    shared = gather_rows(grad_proj[None, :, query_width:].astype(BF16)).astype(F32)
    copies = shared.reshape(KEY_VALUE_HEADS, n_rows // KEY_VALUE_HEADS, *shared.shape[1:])
    heads_sum = jnp.sum(copies, axis=1)
    key_sum = jnp.transpose(heads_sum[:, :, :head_dim], (1, 0, 2)).reshape(key_weight.shape)
    value_sum = jnp.transpose(heads_sum[:, :, head_dim : 2 * head_dim], (1, 0, 2)).reshape(
        value_weight.shape
    )
    gains = jnp.sum(heads_sum[:, :, 2 * head_dim :], axis=0)
    return (
        jnp.stack(results),
        jnp.stack(grad_inputs),
        gains[:, 0],
        grad_proj[:, :query_width],
        key_sum,
        value_sum,
        grad_out.T,
        gains[:, 1],
        grad_gu[:, :ffn_width],
        grad_gu[:, ffn_width:],
        grad_down.T,
    )


def solution(mesh):
    in_specs = (
        P(None, "rows", "cols"),
        P(None, "cols", None),
        P("cols"),
        P("cols", "rows"),
        P("cols", None),
        P("cols", None),
        P("rows", "cols"),
        P("cols"),
        P("cols", "rows"),
        P("cols", "rows"),
        P("rows", "cols"),
        P(None, "rows", "cols"),
    )
    out_specs = (
        P(None, "rows", "cols"),
        P(None, "rows", "cols"),
        P("cols"),
        P("cols", "rows"),
        P("cols", None),
        P("cols", None),
        P("rows", "cols"),
        P("cols"),
        P("cols", "rows"),
        P("cols", "rows"),
        P("rows", "cols"),
    )
    return jax.shard_map(local, mesh=mesh, in_specs=in_specs, out_specs=out_specs, check_vma=False)
```

time: 5170 us -> 1810 us (0.35)
  waiting for transfers between devices: 4360 us -> 996 us
  blocking collectives: 104 us -> 217 us
  local copies, waits for them, and re-layouts: 142 us -> 83.7 us
  matrix products: 385 us -> 333 us
    reduce_scatter x16 -> x12, waiting for transfers between devices: 3040 us -> 432 us  [the longest x8 355 us: scatter_rows(): lax.psum_scatter(partial_sum, 'rows', scatter_dimension=0, tiled=True)]
    all_gather x16 -> x13, waiting for transfers between devices: 1280 us -> 429 us  [the longest x9 316 us: gather_rows(): return lax.all_gather(part, 'rows', axis=0, tiled=True)]
    all_to_all x0 -> x8, blocking collectives: none -> 217 us  [the longest x4 137 us: to_tokens(): lead = lax.all_to_all(lead, 'cols', 0, 0, tiled=True)]
    all_to_all x0 -> x8, waiting for transfers between devices: none -> 132 us  [the longest x3 97.4 us: from_tokens(): lead = lax.all_to_all(lead, 'cols', 0, 0, tiled=True)]
    psum x9 -> x0, blocking collectives: 104 us -> none  [the longest x4 46.7 us: norm_backward(): row_dots = lax.psum(jnp.sum(scaled * normed_input, axis=1), 'cols')]
    dynamic_update_slice x26 -> x0, local copies, waits for them, and re-layouts: 71.8 us -> none  [the longest x12 69.8 us: attention_backward(): lax.scan(one_block, (zeros_kv, zeros_kv), (jnp.arange(block_count, dtype=...]
    dot_general x66 -> x60, matrix products: 385 us -> 333 us  [the longest x8 80.1 us: dot_tn(): lax.dot_general(left_side, right_side, (((0,), (0,)), ((), ())), preferre...]
  transfers between devices with their start and end apart: 33 -> 33, of which waited for: 33 -> 28; matrix products, arithmetic and copies ran while one was open for 8% -> 13% of each run, Pallas kernels for 0% -> 0%
where the time goes in v1:
time: 1810 us
  waiting for transfers between devices  996 us (55%)
  matrix products  333 us (18%)
  blocking collectives  217 us (12%)
  other arithmetic  124 us (7%)
  local copies, waits for them, and re-layouts  83.7 us (5%)
  starting transfers between devices  36 us (2%)
    reduce_scatter x8, waiting for transfers between devices, scatter_rows(): lax.psum_scatter(partial_sum, 'rows', scatter_dimension=0, tiled=True)  355 us
    all_gather x9, waiting for transfers between devices, gather_rows(): return lax.all_gather(part, 'rows', axis=0, tiled=True)  316 us
    all_to_all x4, blocking collectives, to_tokens(): lead = lax.all_to_all(lead, 'cols', 0, 0, tiled=True)  137 us
    all_gather x4, waiting for transfers between devices, gather_cols(): return lax.all_gather(part, 'cols', axis=0, tiled=True)  113 us
    all_to_all x3, waiting for transfers between devices, from_tokens(): lead = lax.all_to_all(lead, 'cols', 0, 0, tiled=True)  97.4 us
    dot_general x8, matrix products, dot_tn(): lax.dot_general(left_side, right_side, (((0,), (0,)), ((), ())), preferre...  80.1 us
    dot_general x8, matrix products, dot_nn(): lax.dot_general(left_side, right_side, (((1,), (0,)), ((), ())), preferre...  79.2 us
    reduce_scatter x4, waiting for transfers between devices, scatter_cols(): lax.psum_scatter(partial_sum.astype(BF16), 'cols', scatter_dimension=0, t...  77.1 us
  transfers between devices with their start and end apart: 33, of which 28 were waited for; matrix products, arithmetic and copies ran while one was open for 13% of the time, Pallas kernels for 0%

profile of v1, /device:TPU:0, one launch (start us, length us, event | category | flops | bytes accessed | tf_op | source)
XLA Modules:
  0.0 1805.4 jit_solution(18115404067205093674)
XLA Ops:
  27.7 45.0 %all_to_all.80 = bf16[4,192,512]{2,1,0:T(8,128)(2,1)S(1)} all-to-all(bf16[4,192,512]{2,1,0:T(8,128)(2,1)S(1)} %bitcast.416), channel_id=1, replica_groups=mesh['rows'=8,'cols'=4] {'cols'}, dimensions={0} | all-to-all | bytes 1572864 | tf_op jit(solution)/shard_map/all_to_all | solution.py:89
  94.5 34.9 %all-gather.17.cloned.1.call-done = bf16[1536,2048]{1,0:T(8,128)(2,1)} async-done(((bf16[192,2048]{1,0:T(8,128)(2,1)}), bf16[1536,2048]{1,0:T(8,128)(2,1)}) %all-gather.17.cloned.1.call-update) | async-done | bytes 6291472 | tf_op jit(solution)/shard_map/all_gather | solution.py:67
  187.3 59.3 %reduce-scatter.13.cloned.1.call-done = bf16[192,2048]{1,0:T(8,128)(2,1)} async-done(((bf16[1536,2048]{1,0:T(8,128)(2,1)}), bf16[192,2048]{1,0:T(8,128)(2,1)}) %reduce-scatter.13.cloned.1.call-update) | async-done | bytes 786448 | tf_op jit(solution)/shard_map/reduce_scatter | solution.py:71
  267.2 45.2 %all_to_all.82 = bf16[4,192,512]{2,1,0:T(8,128)(2,1)S(1)} all-to-all(bf16[4,192,512]{2,1,0:T(8,128)(2,1)S(1)} %bitcast.420), channel_id=1, replica_groups=mesh['rows'=8,'cols'=4] {'cols'}, dimensions={0} | all-to-all | bytes 1572864 | tf_op jit(solution)/shard_map/all_to_all | solution.py:89
  313.4 58.5 %all-gather.23.cloned.1.call-done = bf16[2048,1408]{0,1:T(8,128)(2,1)} async-done(((bf16[512,1408]{0,1:T(8,128)(2,1)}), bf16[2048,1408]{0,1:T(8,128)(2,1)}) %all-gather.23.cloned.1.call-update) | async-done | bytes 5767184 | tf_op jit(solution)/shard_map/all_gather | solution.py:75
  371.9 45.9 %all-gather.21.cloned.1.call-done = bf16[1536,2048]{1,0:T(8,128)(2,1)} async-done(((bf16[192,2048]{1,0:T(8,128)(2,1)}), bf16[1536,2048]{1,0:T(8,128)(2,1)}) %all-gather.21.cloned.1.call-update) | async-done | bytes 6291472 | tf_op jit(solution)/shard_map/all_gather | solution.py:67
  417.9 15.1 fusion.248
  433.0 45.6 %all-gather.25.cloned.1.call-done = bf16[2048,704]{0,1:T(8,128)(2,1)} async-done(((bf16[512,704]{0,1:T(8,128)(2,1)}), bf16[2048,704]{0,1:T(8,128)(2,1)}) %all-gather.25.cloned.1.call-update) | async-done | bytes 2883600 | tf_op jit(solution)/shard_map/all_gather | solution.py:75
  478.6 46.0 %all-gather.31.cloned.1.call-done = bf16[1536,2048]{1,0:T(8,128)(2,1)} async-done(((bf16[192,2048]{1,0:T(8,128)(2,1)}), bf16[1536,2048]{1,0:T(8,128)(2,1)}) %all-gather.31.cloned.1.call-update) | async-done | bytes 6291472 | tf_op jit(solution)/shard_map/all_gather | solution.py:67
  554.4 61.8 %reduce-scatter.21.cloned.1.call-done = bf16[192,2048]{1,0:T(8,128)(2,1)} async-done(((bf16[1536,2048]{1,0:T(8,128)(2,1)}), bf16[192,2048]{1,0:T(8,128)(2,1)}) %reduce-scatter.21.cloned.1.call-update) | async-done | bytes 786448 | tf_op jit(solution)/shard_map/reduce_scatter | solution.py:71
  621.4 45.4 %all-gather.33.cloned.1.call-done = bf16[1536,2048]{1,0:T(8,128)(2,1)} async-done(((bf16[192,2048]{1,0:T(8,128)(2,1)}), bf16[1536,2048]{1,0:T(8,128)(2,1)}) %all-gather.33.cloned.1.call-update) | async-done | bytes 6291472 | tf_op jit(solution)/shard_map/all_gather | solution.py:67
  756.8 24.2 %all_to_all.84 = bf16[4,192,512]{2,1,0:T(8,128)(2,1)S(1)} all-to-all(bf16[4,192,512]{2,1,0:T(8,128)(2,1)S(1)} %bitcast.422), channel_id=1, replica_groups=mesh['rows'=8,'cols'=4] {'cols'}, dimensions={0} | all-to-all | bytes 1572864 | tf_op jit(solution)/shard_map/all_to_all | solution.py:89
  781.7 20.9 %reduce-scatter.23.cloned.1.call-done = bf16[192,2048]{1,0:T(8,128)(2,1)} async-done(((bf16[1536,2048]{1,0:T(8,128)(2,1)}), bf16[192,2048]{1,0:T(8,128)(2,1)}) %reduce-scatter.23.cloned.1.call-update) | async-done | bytes 786448 | tf_op jit(solution)/shard_map/reduce_scatter | solution.py:71
  806.8 44.6 %all-gather.27.cloned.1.call-done = bf16[1536,2048]{1,0:T(8,128)(2,1)} async-done(((bf16[192,2048]{1,0:T(8,128)(2,1)}), bf16[1536,2048]{1,0:T(8,128)(2,1)}) %all-gather.27.cloned.1.call-update) | async-done | bytes 6291472 | tf_op jit(solution)/shard_map/all_gather | solution.py:67
  919.0 52.1 %reduce-scatter.17.cloned.1.call-done = bf16[192,2048]{1,0:T(8,128)(2,1)} async-done(((bf16[1536,2048]{1,0:T(8,128)(2,1)}), bf16[192,2048]{1,0:T(8,128)(2,1)}) %reduce-scatter.17.cloned.1.call-update) | async-done | bytes 786448 | tf_op jit(solution)/shard_map/reduce_scatter | solution.py:71
  972.5 63.6 %reduce-scatter.15.cloned.1.call-done = bf16[192,2048]{1,0:T(8,128)(2,1)} async-done(((bf16[1536,2048]{1,0:T(8,128)(2,1)}), bf16[192,2048]{1,0:T(8,128)(2,1)}) %reduce-scatter.15.cloned.1.call-update) | async-done | bytes 786448 | tf_op jit(solution)/shard_map/reduce_scatter | solution.py:71
  1041.0 21.2 %all_to_all.85 = bf16[8,96,512]{2,1,0:T(8,128)(2,1)S(1)} all-to-all(bf16[8,96,512]{2,1,0:T(8,128)(2,1)} %bitcast.426), channel_id=1, replica_groups=mesh['rows'=8,'cols'=4] {'rows'}, dimensions={0} | all-to-all | bytes 1572864 | tf_op jit(solution)/shard_map/all_to_all | solution.py:87
  1062.2 22.5 %all_to_all.86 = bf16[4,192,512]{2,1,0:T(8,128)(2,1)S(1)} all-to-all(bf16[4,192,512]{2,1,0:T(8,128)(2,1)S(1)} %bitcast.423), channel_id=1, replica_groups=mesh['rows'=8,'cols'=4] {'cols'}, dimensions={0} | all-to-all | bytes 1572864 | tf_op jit(solution)/shard_map/all_to_all | solution.py:89
  1090.8 15.1 fusion.249
  1105.9 32.6 %all-gather.35.cloned.1.call-done = bf16[1536,2048]{1,0:T(8,128)(2,1)} async-done(((bf16[192,2048]{1,0:T(8,128)(2,1)}), bf16[1536,2048]{1,0:T(8,128)(2,1)}) %all-gather.35.cloned.1.call-update) | async-done | bytes 6291472 | tf_op jit(solution)/shard_map/all_gather | solution.py:67
  1168.1 61.8 %reduce-scatter.25.cloned.1.call-done = bf16[192,2048]{1,0:T(8,128)(2,1)} async-done(((bf16[1536,2048]{1,0:T(8,128)(2,1)}), bf16[192,2048]{1,0:T(8,128)(2,1)}) %reduce-scatter.25.cloned.1.call-update) | async-done | bytes 786448 | tf_op jit(solution)/shard_map/reduce_scatter | solution.py:71
  1235.1 45.4 %all-gather.37.cloned.1.call-done = bf16[1536,2048]{1,0:T(8,128)(2,1)} async-done(((bf16[192,2048]{1,0:T(8,128)(2,1)}), bf16[1536,2048]{1,0:T(8,128)(2,1)}) %all-gather.37.cloned.1.call-update) | async-done | bytes 6291472 | tf_op jit(solution)/shard_map/all_gather | solution.py:67
  1383.6 35.9 %reduce-scatter.27.cloned.1.call-done = bf16[192,2048]{1,0:T(8,128)(2,1)} async-done(((bf16[1536,2048]{1,0:T(8,128)(2,1)}), bf16[192,2048]{1,0:T(8,128)(2,1)}) %reduce-scatter.27.cloned.1.call-update) | async-done | bytes 786448 | tf_op jit(solution)/shard_map/reduce_scatter | solution.py:71
  1443.4 16.5 fusion.32
  1459.9 17.6 add_convert_fusion
  1483.9 33.5 %all-to-all-done.2 = bf16[4,192,512]{2,1,0:T(8,128)(2,1)} async-done(((bf16[4,192,512]{2,1,0:T(8,128)(2,1)}), bf16[4,192,512]{2,1,0:T(8,128)(2,1)}, u32[]{:S(2)}, u32[]{:S(2)}) %all-to-all-start.2) | async-done | bytes 786464 | tf_op jit(solution)/shard_map/all_to_all | solution.py:96
  1517.4 28.7 %all_to_all.87 = bf16[4,192,512]{2,1,0:T(8,128)(2,1)} all-to-all(bf16[4,192,512]{2,1,0:T(8,128)(2,1)S(1)} %bitcast.419), channel_id=1, replica_groups=mesh['rows'=8,'cols'=4] {'cols'}, dimensions={0} | all-to-all | bytes 1572864 | tf_op jit(solution)/shard_map/all_to_all | solution.py:96
  1591.9 25.2 %all-to-all-done.6 = bf16[4,192,512]{2,1,0:T(8,128)(2,1)} async-done(((bf16[4,192,512]{2,1,0:T(8,128)(2,1)}), bf16[4,192,512]{2,1,0:T(8,128)(2,1)}, u32[]{:S(2)}, u32[]{:S(2)}) %all-to-all-start.6) | async-done | bytes 786464 | tf_op jit(solution)/shard_map/all_to_all | solution.py:96
  1623.0 38.7 %all-to-all-done.14 = bf16[4,192,512]{2,1,0:T(8,128)(2,1)} async-done(((bf16[4,192,512]{2,1,0:T(8,128)(2,1)}), bf16[4,192,512]{2,1,0:T(8,128)(2,1)}, u32[]{:S(2)}, u32[]{:S(2)}) %all-to-all-start.14) | async-done | bytes 786464 | tf_op jit(solution)/shard_map/all_to_all | solution.py:96
  1682.4 48.3 %reduce-scatter.33.cloned.1.call-done = bf16[512,1408]{1,0:T(8,128)(2,1)} async-done(((bf16[2048,1408]{1,0:T(8,128)(2,1)}), bf16[512,1408]{1,0:T(8,128)(2,1)}) %reduce-scatter.33.cloned.1.call-update) | async-done | bytes 1441808 | tf_op jit(solution)/shard_map/reduce_scatter | solution.py:79
  1735.7 28.7 %reduce-scatter.31.cloned.1.call-done = bf16[512,256]{1,0:T(8,128)(2,1)} async-done(((bf16[2048,256]{1,0:T(8,128)(2,1)}), bf16[512,256]{1,0:T(8,128)(2,1)}) %reduce-scatter.31.cloned.1.call-update) | async-done | bytes 262160 | tf_op jit(solution)/shard_map/reduce_scatter | solution.py:79
  1773.1 16.0 all-gather.39.cloned.1.call-done
  (504 shorter events, 593.2 us)
Async XLA Ops:
  9.9 17.8 all-to-all-start
  15.1 67.2 %all-gather.15.cloned.1.call-start = ((), (), s32[]{:S(2)}) async-start(), calls=%async_computation.28 | async-start | bytes 2621440 | tf_op jit(solution)/shard_map/all_gather | solution.py:75
  16.7 112.7 %all-gather.17.cloned.1.call-start = ((), (), s32[]{:S(2)}) async-start(), calls=%async_computation.29 | async-start | bytes 7077888 | tf_op jit(solution)/shard_map/all_gather | solution.py:67
  85.2 93.6 %all-gather.19.cloned.1.call-start = ((), (), s32[]{:S(2)}) async-start(), calls=%async_computation.30 | async-start | bytes 1310720 | tf_op jit(solution)/shard_map/all_gather | solution.py:75
  85.9 160.7 %reduce-scatter.13.cloned.1.call-start = ((), (), s32[]{:S(2)}) async-start(), calls=%async_computation.31 | async-start | bytes 7077888 | tf_op jit(solution)/shard_map/reduce_scatter | solution.py:71
  184.7 187.2 %all-gather.23.cloned.1.call-start = ((), (), s32[]{:S(2)}) async-start(), calls=%async_computation.33 | async-start | bytes 7208960 | tf_op jit(solution)/shard_map/all_gather | solution.py:75
  187.2 230.6 %all-gather.21.cloned.1.call-start = ((), (), s32[]{:S(2)}) async-start(), calls=%async_computation.32 | async-start | bytes 7077888 | tf_op jit(solution)/shard_map/all_gather | solution.py:67
  250.3 228.2 %all-gather.25.cloned.1.call-start = ((), (), s32[]{:S(2)}) async-start(), calls=%async_computation.34 | async-start | bytes 3604480 | tf_op jit(solution)/shard_map/all_gather | solution.py:75
  251.1 273.5 %all-gather.31.cloned.1.call-start = ((), (), s32[]{:S(2)}) async-start(), calls=%async_computation.40 | async-start | bytes 7077888 | tf_op jit(solution)/shard_map/all_gather | solution.py:67
  313.4 302.8 %reduce-scatter.21.cloned.1.call-start = ((), (), s32[]{:S(2)}) async-start(), calls=%async_computation.41 | async-start | bytes 7077888 | tf_op jit(solution)/shard_map/reduce_scatter | solution.py:71
  554.3 112.5 %all-gather.33.cloned.1.call-start = ((), (), s32[]{:S(2)}) async-start(), calls=%async_computation.42 | async-start | bytes 7077888 | tf_op jit(solution)/shard_map/all_gather | solution.py:67
  621.2 181.3 %reduce-scatter.23.cloned.1.call-start = ((), (), s32[]{:S(2)}) async-start(), calls=%async_computation.43 | async-start | bytes 7077888 | tf_op jit(solution)/shard_map/reduce_scatter | solution.py:71
  740.6 110.7 %all-gather.27.cloned.1.call-start = ((), (), s32[]{:S(2)}) async-start(), calls=%async_computation.36 | async-start | bytes 7077888 | tf_op jit(solution)/shard_map/all_gather | solution.py:67
  805.8 165.3 %reduce-scatter.17.cloned.1.call-start = ((), (), s32[]{:S(2)}) async-start(), calls=%async_computation.37 | async-start | bytes 7077888 | tf_op jit(solution)/shard_map/reduce_scatter | solution.py:71
  909.2 126.9 %reduce-scatter.15.cloned.1.call-start = ((), (), s32[]{:S(2)}) async-start(), calls=%async_computation.35 | async-start | bytes 7077888 | tf_op jit(solution)/shard_map/reduce_scatter | solution.py:71
  918.3 172.5 %all-gather.29.cloned.1.call-start = ((), (), s32[]{:S(2)}) async-start(), calls=%async_computation.38 | async-start | bytes 7077888 | tf_op jit(solution)/shard_map/all_gather | solution.py:67
  1040.9 97.6 %all-gather.35.cloned.1.call-start = ((), (), s32[]{:S(2)}) async-start(), calls=%async_computation.44 | async-start | bytes 7077888 | tf_op jit(solution)/shard_map/all_gather | solution.py:67
  1085.7 144.2 %reduce-scatter.25.cloned.1.call-start = ((), (), s32[]{:S(2)}) async-start(), calls=%async_computation.45 | async-start | bytes 7077888 | tf_op jit(solution)/shard_map/reduce_scatter | solution.py:71
  1168.0 112.5 %all-gather.37.cloned.1.call-start = ((), (), s32[]{:S(2)}) async-start(), calls=%async_computation.46 | async-start | bytes 7077888 | tf_op jit(solution)/shard_map/all_gather | solution.py:67
  1235.0 184.5 %reduce-scatter.27.cloned.1.call-start = ((), (), s32[]{:S(2)}) async-start(), calls=%async_computation.47 | async-start | bytes 7077888 | tf_op jit(solution)/shard_map/reduce_scatter | solution.py:71
  1357.5 210.0 %reduce-scatter.19.cloned.1.call-start = ((), (), s32[]{:S(2)}) async-start(), calls=%async_computation.39 | async-start | bytes 7077888 | tf_op jit(solution)/shard_map/reduce_scatter | solution.py:71
  1366.8 254.5 %reduce-scatter.29.cloned.1.call-start = ((), (), s32[]{:S(2)}) async-start(), calls=%async_computation.48 | async-start | bytes 2007040 | tf_op jit(solution)/shard_map/reduce_scatter | solution.py:79
  1425.7 239.9 %reduce-scatter.35.cloned.1.call-start = ((), (), s32[]{:S(2)}) async-start(), calls=%async_computation.51 | async-start | bytes 3604480 | tf_op jit(solution)/shard_map/reduce_scatter | solution.py:79
  1443.3 287.4 %reduce-scatter.33.cloned.1.call-start = ((), (), s32[]{:S(2)}) async-start(), calls=%async_computation.50 | async-start | bytes 7208960 | tf_op jit(solution)/shard_map/reduce_scatter | solution.py:79
  1479.6 37.8 %all-to-all-start.2 = ((bf16[4,192,512]{2,1,0:T(8,128)(2,1)}), bf16[4,192,512]{2,1,0:T(8,128)(2,1)}, u32[]{:S(2)}, u32[]{:S(2)}) async-start(bf16[4,192,512]{2,1,0:T(8,128)(2,1)} %bitcast.418), calls=%async_computation.4 | async-start | bytes 1572864 | tf_op jit(solution)/shard_map/all_to_all | solution.py:96
  1546.2 16.8 all-to-all-start.3
  1563.0 17.1 all-to-all-start.11
  1580.0 37.0 %all-to-all-start.6 = ((bf16[4,192,512]{2,1,0:T(8,128)(2,1)}), bf16[4,192,512]{2,1,0:T(8,128)(2,1)}, u32[]{:S(2)}, u32[]{:S(2)}) async-start(bf16[4,192,512]{2,1,0:T(8,128)(2,1)} %bitcast.355), calls=%async_computation.10 | async-start | bytes 1572864 | tf_op jit(solution)/shard_map/all_to_all | solution.py:96
  1584.3 180.1 %reduce-scatter.31.cloned.1.call-start = ((), (), s32[]{:S(2)}) async-start(), calls=%async_computation.49 | async-start | bytes 1310720 | tf_op jit(solution)/shard_map/reduce_scatter | solution.py:79
  1617.1 44.6 %all-to-all-start.14 = ((bf16[4,192,512]{2,1,0:T(8,128)(2,1)}), bf16[4,192,512]{2,1,0:T(8,128)(2,1)}, u32[]{:S(2)}, u32[]{:S(2)}) async-start(bf16[4,192,512]{2,1,0:T(8,128)(2,1)} %bitcast.351), calls=%async_computation.22 | async-start | bytes 1572864 | tf_op jit(solution)/shard_map/all_to_all | solution.py:96
  1621.3 167.8 %all-gather.39.cloned.1.call-start = ((), (), s32[]{:S(2)}) async-start(), calls=%async_computation.52 | async-start | bytes 1253376 | tf_op jit(solution)/shard_map/all_gather | solution.py:67
  1678.2 90.7 %all-to-all-start.15 = ((bf16[8,96,512]{2,1,0:T(8,128)(2,1)}), bf16[8,96,512]{2,1,0:T(8,128)(2,1)}, u32[]{:S(2)}, u32[]{:S(2)}) async-start(bf16[8,96,512]{2,1,0:T(8,128)(2,1)} %bitcast.102), calls=%async_computation.23 | async-start | bytes 1572864 | tf_op jit(solution)/shard_map/all_to_all | solution.py:98
  (115 other events, 3913.6 us)
Sparse Core Ops, SparseCore 0:
  18.1 64.2 all-gather.14
  85.3 44.0 all-gather.16
  131.0 27.9 all-gather.18
  184.8 61.7 reduce-scatter.12
  248.6 123.3 all-gather.22
  374.3 43.5 all-gather.20
  419.4 59.0 all-gather.24
  480.4 44.0 all-gather.30
  554.4 61.7 reduce-scatter.20
  621.4 45.3 all-gather.32
  740.7 61.7 reduce-scatter.22
  805.9 45.3 all-gather.26
  909.3 61.7 reduce-scatter.16
  974.3 61.7 reduce-scatter.14
  1041.1 49.7 all-gather.28
  1093.1 45.3 all-gather.34
  1168.1 61.7 reduce-scatter.24
  1235.1 45.3 all-gather.36
  1357.6 61.7 reduce-scatter.26
  1422.7 61.7 reduce-scatter.18
  1486.7 48.0 reduce-scatter.28
  1537.7 75.2 reduce-scatter.34
  1615.4 115.3 reduce-scatter.32
  1733.5 30.8 reduce-scatter.30
  1766.8 22.2 all-gather.38
